TPU v7x, 32 devices: a whole 2x2x4 slice. The times are simulated.
32 devices in a mesh: row: 4 (over y, x), col: 8 (over z, core).
Axes of the slice: x: 2, y: 2, z: 4, core: 2. Of those that a mesh axis runs over, the one named last changes fastest.
Arguments:
- layer_input: bfloat16 [8192, 2048], P(('row', 'col')), may hold values from -6 to 6
- out_grad: bfloat16 [8192, 2048], P(('row', 'col')), may hold values from -6 to 6
- kv_grad: bfloat16 [8192, 256], P(('row', 'col')), may hold values from -6 to 6
- lengths: int32 [4, 4], P('row'), may hold values from 1 to 1024, 2048 in all within a row
- token_deal: int32 [4, 2048], P('row'), may hold values from 0 to 2047, each once within a row
- attn_gain: float32 [2048], P('row'), may hold values from 0.25 to 1.75
- query_weight: float32 [2048, 2048], P('row', 'col'), may hold values from -0.125 to 0.125
- key_weight: float32 [2048, 128], P('row'), may hold values from -0.125 to 0.125
- value_weight: float32 [2048, 128], P('row'), may hold values from -0.125 to 0.125
- out_weight: float32 [2048, 2048], P('col', 'row'), may hold values from -1 to 1
- mlp_gain: float32 [2048], P('row'), may hold values from 0.25 to 1.75
- gate_weight: float32 [2048, 5632], P('row', 'col'), may hold values from -0.125 to 0.125
- up_weight: float32 [2048, 5632], P('row', 'col'), may hold values from -0.125 to 0.125
- down_weight: float32 [5632, 2048], P('col', 'row'), may hold values from -0.3125 to 0.3125
Outputs:
- layer_output: bfloat16 [8192, 2048], P(('row', 'col'))
- input_grad: float32 [8192, 2048], P(('row', 'col'))
- shared_kv: bfloat16 [8192, 256], P(('row', 'col'))
- attn_gain_grad: float32 [2048], P('row')
- query_weight_grad: float32 [2048, 2048], P('row', 'col')
- key_weight_grad: float32 [2048, 128], P('row')
- value_weight_grad: float32 [2048, 128], P('row')
- out_weight_grad: float32 [2048, 2048], P('col', 'row')
- mlp_gain_grad: float32 [2048], P('row')
- gate_weight_grad: float32 [2048, 5632], P('row', 'col')
- up_weight_grad: float32 [2048, 5632], P('row', 'col')
- down_weight_grad: float32 [5632, 2048], P('col', 'row')
Inputs may be any that keep to these rules, and one draw needn't show every extreme that they name: Each row holds 4 lengths that sum to 2048; the longest of each row is exactly 1024. `token_deal`: each row is a permutation of 0 to 2047.
All inputs are finite; a program needn't handle non-finite values.
Results may differ from a plain program's by a relative error of at most 0.017.
The roundings to bfloat16 on the way count: a program that leaves them out, or rounds other values in their place, can miss the bound.
Values may be sent and summed in bfloat16 or wider, within the bound.
No kernel may reach another device: no remote copies, remote signals or barrier semaphores. Data moves between devices by JAX's collectives and lax.ppermute only.
A program may use at most 320 MiB of HBM per device.

v0:
```python
import jax
import jax.numpy as jnp
from jax import lax
from jax.sharding import PartitionSpec as P

norm_eps = 1e-05
rope_base = 10000.0
masked_score = -1e30


def rotate_pairs(values, positions, direction):
    half_dim = values.shape[-1] // 2
    frequency = rope_base ** (-jnp.arange(half_dim, dtype=jnp.float32) / half_dim)
    angles = positions.astype(jnp.float32)[:, None, None] * frequency
    cosine = jnp.cos(angles)
    sine_part = jnp.sin(angles) * direction
    first_half = values[..., :half_dim]
    second = values[..., half_dim:]
    return jnp.concatenate(
        [first_half * cosine - second * sine_part, second * cosine + first_half * sine_part],
        axis=-1,
    )


def norm_parts(values, gain):
    factor = lax.rsqrt(jnp.mean(values * values, axis=-1, keepdims=True) + norm_eps)
    return (factor, values * factor * gain)


def norm_backward(values, factor, gain, grad_rows):
    weighted = grad_rows * gain
    inner_mean = jnp.mean(weighted * values, axis=-1, keepdims=True)
    input_part = factor * weighted - values * factor * factor * factor * inner_mean
    gain_part = jnp.sum(grad_rows * values * factor, axis=0)
    return (input_part, gain_part)


def sequence_info(seq_lengths, group_rows):
    positions = jnp.arange(group_rows, dtype=jnp.int32)
    seq_ends = jnp.cumsum(seq_lengths)
    seq_ids = jnp.sum((positions[:, None] >= seq_ends[None, :]).astype(jnp.int32), axis=1)
    starts = jnp.sum(
        jnp.where(seq_ends[None, :] <= positions[:, None], seq_lengths[None, :], 0), axis=1
    )
    return (positions, seq_ids, positions - starts)


def block_scores(query_block, key_rows, seq_ids, first_row, block_rows, score_scale):
    key_index = jnp.arange(key_rows.shape[0], dtype=jnp.int32)
    row_index = first_row + jnp.arange(block_rows, dtype=jnp.int32)
    row_seq = lax.dynamic_slice_in_dim(seq_ids, first_row, block_rows, 0)
    scores = (
        jnp.einsum("qhd,kd->hqk", query_block, key_rows, preferred_element_type=jnp.float32)
        * score_scale
    )
    allowed = (row_seq[:, None] == seq_ids[None, :]) & (key_index[None, :] <= row_index[:, None])
    return jnp.where(allowed[None], scores, masked_score)


def attend_forward(queries, key_rows, value_rows, seq_ids):
    group_rows, head_count, head_dim = queries.shape
    block_rows = min(512, group_rows)
    score_scale = float(head_dim) ** (-0.5)
    count_blocks = group_rows // block_rows
    query_blocks = queries.reshape(count_blocks, block_rows, head_count, head_dim)
    first_rows = jnp.arange(count_blocks, dtype=jnp.int32) * block_rows

    def one_block(pieces):
        query_block, first_row = pieces
        scores = block_scores(query_block, key_rows, seq_ids, first_row, block_rows, score_scale)
        highest = jnp.max(scores, axis=-1, keepdims=True)
        exponent = jnp.exp(scores - highest)
        row_total = jnp.sum(exponent, axis=-1, keepdims=True)
        prob_low = (exponent / row_total).astype(jnp.bfloat16)
        mixed_rows = jnp.einsum(
            "hqk,kd->qhd", prob_low, value_rows, preferred_element_type=jnp.float32
        )
        return (mixed_rows.astype(jnp.bfloat16), (highest + jnp.log(row_total))[..., 0])

    mixed_rows, log_norm = lax.map(one_block, (query_blocks, first_rows))
    return (mixed_rows.reshape(group_rows, head_count, head_dim), log_norm)


def attend_backward(queries, key_rows, value_rows, seq_ids, mixed_grad, log_norm):
    group_rows, head_count, head_dim = queries.shape
    block_rows = min(512, group_rows)
    score_scale = float(head_dim) ** (-0.5)
    count_blocks = group_rows // block_rows
    query_blocks = queries.reshape(count_blocks, block_rows, head_count, head_dim)
    grad_blocks = mixed_grad.reshape(count_blocks, block_rows, head_count, head_dim)
    first_rows = jnp.arange(count_blocks, dtype=jnp.int32) * block_rows

    def one_block(carry, pieces):
        key_grad, value_grad = carry
        query_block, grad_block, norm_block, first_row = pieces
        scores = block_scores(query_block, key_rows, seq_ids, first_row, block_rows, score_scale)
        softmax_rows = jnp.exp(scores - norm_block[..., None])
        prob_low = softmax_rows.astype(jnp.bfloat16)
        prob_grad = jnp.einsum(
            "qhd,kd->hqk", grad_block, value_rows, preferred_element_type=jnp.float32
        )
        row_dot = jnp.sum(softmax_rows * prob_grad, axis=-1, keepdims=True)
        score_grad = (softmax_rows * (prob_grad - row_dot)).astype(jnp.bfloat16)
        query_grad = (
            jnp.einsum("hqk,kd->qhd", score_grad, key_rows, preferred_element_type=jnp.float32)
            * score_scale
        )
        key_grad = (
            key_grad
            + jnp.einsum("hqk,qhd->kd", score_grad, query_block, preferred_element_type=jnp.float32)
            * score_scale
        )
        value_grad = value_grad + jnp.einsum(
            "hqk,qhd->kd", prob_low, grad_block, preferred_element_type=jnp.float32
        )
        return ((key_grad, value_grad), query_grad)

    zero_rows = jnp.zeros((group_rows, head_dim), jnp.float32)
    (key_grad, value_grad), query_grad = lax.scan(
        one_block, (zero_rows, zero_rows), (query_blocks, grad_blocks, log_norm, first_rows)
    )
    return (query_grad.reshape(group_rows, head_count, head_dim), key_grad, value_grad)


def local(
    layer_input,
    out_grad,
    kv_grad,
    lengths,
    token_deal,
    attn_gain,
    query_weight,
    key_weight,
    value_weight,
    out_weight,
    mlp_gain,
    gate_weight,
    up_weight,
    down_weight,
):
    own_rows = layer_input.shape[0]
    col_index = lax.axis_index("col")
    group_rows = own_rows * lax.axis_size("col")
    head_dim = key_weight.shape[1]
    (
        gain_one,
        query_copy,
        key_copy,
        value_copy,
        out_copy,
        gain_two,
        gate_copy,
        up_copy,
        down_copy,
    ) = (
        lax.all_gather(attn_gain.astype(jnp.bfloat16), "row", axis=0, tiled=True),
        lax.all_gather(query_weight.astype(jnp.bfloat16), "row", axis=0, tiled=True),
        lax.all_gather(key_weight.astype(jnp.bfloat16), "row", axis=0, tiled=True),
        lax.all_gather(value_weight.astype(jnp.bfloat16), "row", axis=0, tiled=True),
        lax.all_gather(out_weight.astype(jnp.bfloat16), "row", axis=1, tiled=True),
        lax.all_gather(mlp_gain.astype(jnp.bfloat16), "row", axis=0, tiled=True),
        lax.all_gather(gate_weight.astype(jnp.bfloat16), "row", axis=0, tiled=True),
        lax.all_gather(up_weight.astype(jnp.bfloat16), "row", axis=0, tiled=True),
        lax.all_gather(down_weight.astype(jnp.bfloat16), "row", axis=1, tiled=True),
    )
    gain_one = gain_one.astype(jnp.float32)
    gain_two = gain_two.astype(jnp.float32)
    head_count = query_copy.shape[1] // head_dim
    positions, seq_ids, within = sequence_info(lengths[0], group_rows)
    slot_order = token_deal[0]
    inverse = jnp.zeros((group_rows,), jnp.int32).at[slot_order].set(positions)
    slot_pos = within[slot_order]
    own_pos = lax.dynamic_slice_in_dim(slot_pos, col_index * own_rows, own_rows, 0)
    input_rows = layer_input.astype(jnp.float32)
    factor_one, normed_one = norm_parts(input_rows, gain_one)
    normed_own = normed_one.astype(jnp.bfloat16)
    normed_rows, grad_rows = (
        lax.all_gather(normed_own, "col", axis=0, tiled=True),
        lax.all_gather(out_grad, "col", axis=0, tiled=True),
    )
    queries = jnp.dot(normed_rows, query_copy, preferred_element_type=jnp.float32).reshape(
        group_rows, head_count, head_dim
    )
    queries = rotate_pairs(queries, slot_pos, 1.0).astype(jnp.bfloat16)
    key_proj = jnp.dot(normed_rows, key_copy, preferred_element_type=jnp.float32)
    key_rows = rotate_pairs(key_proj[:, None, :], slot_pos, 1.0)[:, 0, :].astype(jnp.bfloat16)
    value_rows = jnp.dot(normed_rows, value_copy, preferred_element_type=jnp.float32).astype(
        jnp.bfloat16
    )
    shared_rows = jnp.concatenate([key_rows, value_rows], axis=1)
    shared_own = lax.dynamic_slice_in_dim(shared_rows, col_index * own_rows, own_rows, 0)
    query_orig = queries[inverse]
    key_orig = key_rows[inverse]
    value_orig = value_rows[inverse]
    mixed_orig, log_norm = attend_forward(query_orig, key_orig, value_orig, seq_ids)
    mixed_slot = mixed_orig[slot_order].reshape(group_rows, head_count * head_dim)
    out_full = lax.all_gather(out_copy, "col", axis=0, tiled=True)
    mixed_own = lax.all_to_all(mixed_slot, "col", split_axis=0, concat_axis=1, tiled=True)
    attended = jnp.dot(mixed_own, out_full, preferred_element_type=jnp.float32)
    middle = input_rows + attended
    factor_two, normed_two = norm_parts(middle, gain_two)
    mlp_rows = lax.all_gather(normed_two.astype(jnp.bfloat16), "col", axis=0, tiled=True)
    gate_act = jnp.dot(mlp_rows, gate_copy, preferred_element_type=jnp.float32)
    upward = jnp.dot(mlp_rows, up_copy, preferred_element_type=jnp.float32)
    sigmoid_gate = jax.nn.sigmoid(gate_act)
    silu_gate = gate_act * sigmoid_gate
    hidden = (silu_gate * upward).astype(jnp.bfloat16)
    output_rows = middle + lax.psum_scatter(
        jnp.dot(hidden, down_copy, preferred_element_type=jnp.float32),
        "col",
        scatter_dimension=0,
        tiled=True,
    )
    hidden_grad = jnp.dot(grad_rows, down_copy.T, preferred_element_type=jnp.float32)
    down_wgrad = jnp.dot(hidden.T, grad_rows, preferred_element_type=jnp.float32)
    gate_grad = (
        hidden_grad * upward * sigmoid_gate * (1.0 + gate_act * (1.0 - sigmoid_gate))
    ).astype(jnp.bfloat16)
    up_grad = (hidden_grad * silu_gate).astype(jnp.bfloat16)
    gate_wgrad = jnp.dot(mlp_rows.T, gate_grad, preferred_element_type=jnp.float32)
    up_wgrad = jnp.dot(mlp_rows.T, up_grad, preferred_element_type=jnp.float32)
    normed_two_grad = lax.psum_scatter(
        jnp.dot(gate_grad, gate_copy.T, preferred_element_type=jnp.float32)
        + jnp.dot(up_grad, up_copy.T, preferred_element_type=jnp.float32),
        "col",
        scatter_dimension=0,
        tiled=True,
    )
    middle_part, gain_two_grad = norm_backward(middle, factor_two, gain_two, normed_two_grad)
    middle_grad = out_grad.astype(jnp.float32) + middle_part
    middle_low = middle_grad.astype(jnp.bfloat16)
    middle_rows = lax.all_gather(middle_low, "col", axis=0, tiled=True)
    mixed_grad_slot = jnp.dot(middle_rows, out_copy.T, preferred_element_type=jnp.float32).astype(
        jnp.bfloat16
    )
    out_wgrad = jnp.dot(mixed_slot.T, middle_rows, preferred_element_type=jnp.float32)
    mixed_grad = mixed_grad_slot.reshape(group_rows, head_count, head_dim)[inverse]
    query_grad, key_grad, value_grad = attend_backward(
        query_orig, key_orig, value_orig, seq_ids, mixed_grad, log_norm
    )
    query_grad = (
        rotate_pairs(query_grad[slot_order], slot_pos, -1.0)
        .astype(jnp.bfloat16)
        .reshape(group_rows, head_count * head_dim)
    )
    query_wgrad = jnp.dot(normed_rows.T, query_grad, preferred_element_type=jnp.float32)
    shared_part = jnp.concatenate([key_grad, value_grad], axis=1)[slot_order]
    shared_cols = shared_part.shape[1]
    grad_parts = jnp.concatenate(
        [jnp.dot(query_grad, query_copy.T, preferred_element_type=jnp.float32), shared_part], axis=1
    )
    summed_parts = lax.psum_scatter(grad_parts, "col", scatter_dimension=0, tiled=True)
    width_cols = summed_parts.shape[1] - shared_cols
    normed_one_grad = summed_parts[:, :width_cols]
    shared_grad = summed_parts[:, width_cols:]
    shared_grad = shared_grad + kv_grad.astype(jnp.float32)
    key_own = rotate_pairs(shared_grad[:, None, :head_dim], own_pos, -1.0)[:, 0, :].astype(
        jnp.bfloat16
    )
    value_own = shared_grad[:, head_dim:].astype(jnp.bfloat16)
    key_wgrad = jnp.dot(normed_own.T, key_own, preferred_element_type=jnp.float32)
    value_wgrad = jnp.dot(normed_own.T, value_own, preferred_element_type=jnp.float32)
    normed_one_grad = (
        normed_one_grad
        + jnp.dot(key_own, key_copy.T, preferred_element_type=jnp.float32)
        + jnp.dot(value_own, value_copy.T, preferred_element_type=jnp.float32)
    )
    input_part, gain_one_grad = norm_backward(input_rows, factor_one, gain_one, normed_one_grad)
    input_grad = middle_grad + input_part
    summed = (
        lax.psum_scatter(gain_one_grad, "row", scatter_dimension=0, tiled=True),
        lax.psum_scatter(query_wgrad, "row", scatter_dimension=0, tiled=True),
        lax.psum_scatter(key_wgrad, "row", scatter_dimension=0, tiled=True),
        lax.psum_scatter(value_wgrad, "row", scatter_dimension=0, tiled=True),
        lax.psum_scatter(out_wgrad, "row", scatter_dimension=1, tiled=True),
        lax.psum_scatter(gain_two_grad, "row", scatter_dimension=0, tiled=True),
        lax.psum_scatter(gate_wgrad, "row", scatter_dimension=0, tiled=True),
        lax.psum_scatter(up_wgrad, "row", scatter_dimension=0, tiled=True),
        lax.psum_scatter(down_wgrad, "row", scatter_dimension=1, tiled=True),
    )
    gain_one_sum, key_sum, value_sum, gain_two_sum = lax.psum(
        (summed[0], summed[2], summed[3], summed[5]), "col"
    )
    return (
        output_rows.astype(jnp.bfloat16),
        input_grad,
        shared_own,
        gain_one_sum,
        summed[1],
        key_sum,
        value_sum,
        summed[4],
        gain_two_sum,
        summed[6],
        summed[7],
        summed[8],
    )


def solution(mesh):
    in_specs = (
        P(("row", "col"), None),
        P(("row", "col"), None),
        P(("row", "col"), None),
        P("row", None),
        P("row", None),
        P("row"),
        P("row", "col"),
        P("row", None),
        P("row", None),
        P("col", "row"),
        P("row"),
        P("row", "col"),
        P("row", "col"),
        P("col", "row"),
    )
    out_specs = (
        P(("row", "col"), None),
        P(("row", "col"), None),
        P(("row", "col"), None),
        P("row"),
        P("row", "col"),
        P("row", None),
        P("row", None),
        P("col", "row"),
        P("row"),
        P("row", "col"),
        P("row", "col"),
        P("col", "row"),
    )
    return jax.shard_map(local, mesh=mesh, in_specs=in_specs, out_specs=out_specs, check_vma=False)
```

profile of v0, /device:TPU:0, one launch (start us, length us, event | category | flops | bytes accessed | tf_op | source)
XLA Modules:
  0.0 1775.5 jit_solution(17734194517630113278)
XLA Ops:
  9.8 9.6 all-gather
  24.0 15.5 all-gather.17.cloned.1.call-done
  40.9 8.0 scatter_custom_fusion
  49.1 11.8 gather_fusion
  61.0 10.1 all_gather.46
  71.1 9.6 all_gather.45
  86.4 37.8 %all-gather.13.cloned.1.call-done = bf16[2048,2048]{0,1:T(8,128)(2,1)} async-done(((bf16[256,2048]{0,1:T(8,128)(2,1)}), bf16[2048,2048]{0,1:T(8,128)(2,1)}) %all-gather.13.cloned.1.call-update) | async-done | bytes 8388624 | tf_op jit(solution)/shard_map/all_gather | solution.py:178
  137.6 6.2 gather_fusion.3
  173.8 13.9 gather_fusion.1
  189.1 50.7 %while.27 = (s32[]{:T(128)}, bf16[4,512,2,128]{3,1,0,2:T(8,128)(2,1)}, f32[4,2,512]{2,1,0:T(2,128)S(1)}, s32[4]{0:T(128)S(1)}, s32[2048]{0:T(1024)S(1)}, /*index...) while((s32[]{:T(128)}, ...), condition=%wide.region_8.9_spmd, body=%wide.region_5.8_spmd.sunk | while | flops 1102183936 | bytes 30984376 | solution.py:80
  243.9 15.1 gather_fusion.4
  268.5 8.2 all-gather.1
  276.7 18.2 %all-to-all-done = bf16[8,256,256]{1,2,0:T(8,128)(2,1)S(1)} async-done(((bf16[8,256,256]{1,2,0:T(8,128)(2,1)}), bf16[8,256,256]{1,2,0:T(8,128)(2,1)S(1)}, u32[]{:S(2)}, u32[]{:S(2)}) %all-to-all-start) | async-done | bytes 1048608 | tf_op jit(solution)/shard_map/all_to_all | solution.py:198
  295.9 7.1 multiply_reduce_fusion.2
  310.7 74.6 %all-gather.21.cloned.1.call-done = bf16[2048,2048]{0,1:T(8,128)(2,1)} async-done(((bf16[256,2048]{0,1:T(8,128)(2,1)}), bf16[2048,2048]{0,1:T(8,128)(2,1)}) %all-gather.21.cloned.1.call-update) | async-done | bytes 8388624 | tf_op jit(solution)/shard_map/all_gather | solution.py:202
  385.3 11.0 fusion.99
  396.3 31.1 %all-gather.25.cloned.1.call-done = bf16[2048,704]{0,1:T(8,128)(2,1)} async-done(((bf16[512,704]{0,1:T(8,128)(2,1)}), bf16[2048,704]{0,1:T(8,128)(2,1)}) %all-gather.25.cloned.1.call-update) | async-done | bytes 2883600 | tf_op jit(solution)/shard_map/all_gather | solution.py:163
  427.4 11.0 fusion.100
  438.5 32.4 %all-gather.27.cloned.1.call-done = bf16[704,2048]{1,0:T(8,128)(2,1)} async-done(((bf16[704,512]{1,0:T(8,128)(2,1)}), bf16[704,2048]{1,0:T(8,128)(2,1)}) %all-gather.27.cloned.1.call-update) | async-done | bytes 2883600 | tf_op jit(solution)/shard_map/all_gather | solution.py:164
  470.8 83.7 %all-gather.29.cloned.1.call-done = bf16[2048,2048]{1,0:T(8,128)(2,1)} async-done(((bf16[256,2048]{1,0:T(8,128)(2,1)}), bf16[2048,2048]{1,0:T(8,128)(2,1)}) %all-gather.29.cloned.1.call-update) | async-done | bytes 8388624 | tf_op jit(solution)/shard_map/all_gather | solution.py:179
  554.5 15.3 multiply_convert_fusion
  569.8 10.4 fusion.94
  580.2 13.8 convolution_add_fusion
  595.7 165.2 %reduce-scatter.13.cloned.1.call-done = f32[256,2048]{0,1:T(8,128)} async-done(((f32[2048,2048]{0,1:T(8,128)}), f32[256,2048]{0,1:T(8,128)}) %reduce-scatter.13.cloned.1.call-update) | async-done | bytes 2097168 | tf_op jit(solution)/shard_map/reduce_scatter | solution.py:222
  765.8 81.0 %all-gather.31.cloned.1.call-done = bf16[2048,2048]{0,1:T(8,128)(2,1)} async-done(((bf16[256,2048]{0,1:T(8,128)(2,1)}), bf16[2048,2048]{0,1:T(8,128)(2,1)}) %all-gather.31.cloned.1.call-update) | async-done | bytes 8388624 | tf_op jit(solution)/shard_map/all_gather | solution.py:232
  846.8 7.0 convolution_convert_fusion
  857.8 15.1 gather_fusion.5
  873.0 77.5 %while.28 = (s32[]{:T(128)}, f32[2048,128]{1,0:T(8,128)S(1)}, f32[2048,128]{1,0:T(8,128)}, f32[4,512,2,128]{3,1,0,2:T(8,128)}, s32[4]{0:T(128)S(1)}, /*index=5*/...) while((s32[]{:T(128)}, f32[2048,128]{1,0:T(8,128)S(1)}, ...), condition=%wide.region_15.16_spmd.clone, body=%wide.region_13.15_spmd.clone.sunk | while | flops 2720398848 | bytes 83409176 | solution.py:119
  955.3 14.5 gather_fusion.6
  971.2 8.6 gather_fusion.7
  982.9 8.9 subtract_convert_fusion
  997.1 8.7 pad_maximum_fusion
  1007.6 184.5 %reduce-scatter.15.cloned.1.call-done = f32[256,2304]{0,1:T(8,128)} async-done(((f32[2048,2304]{0,1:T(8,128)}), f32[256,2304]{0,1:T(8,128)}) %reduce-scatter.15.cloned.1.call-update) | async-done | bytes 2359312 | tf_op jit(solution)/shard_map/reduce_scatter | solution.py:252
  1196.5 12.7 fusion.93
  1209.2 11.2 fusion.98
  1220.5 11.2 fusion.96
  1231.8 11.1 fusion.97
  1243.2 7.3 fusion.59
  1252.6 7.5 fusion.95
  1267.7 154.9 %reduce-scatter.11.cloned.1.call-done = f32[256,2048]{0,1:T(8,128)} async-done(((f32[2048,2048]{0,1:T(8,128)}), f32[256,2048]{0,1:T(8,128)}) %reduce-scatter.11.cloned.1.call-update) | async-done | bytes 2097168 | tf_op jit(solution)/shard_map/reduce_scatter | solution.py:208
  1427.5 17.1 all-reduce.4
  1449.1 14.2 all-reduce.2
  1463.3 27.2 %reduce-scatter.29.cloned.1.call-done = f32[704,512]{1,0:T(8,128)} async-done(((f32[704,2048]{1,0:T(8,128)}), f32[704,512]{1,0:T(8,128)}) %reduce-scatter.29.cloned.1.call-update) | async-done | bytes 1441808 | tf_op jit(solution)/shard_map/reduce_scatter | solution.py:279
  1490.4 69.1 %reduce-scatter.25.cloned.1.call-done = f32[512,704]{0,1:T(8,128)} async-done(((f32[2048,704]{0,1:T(8,128)}), f32[512,704]{0,1:T(8,128)}) %reduce-scatter.25.cloned.1.call-update) | async-done | bytes 1441808 | tf_op jit(solution)/shard_map/reduce_scatter | solution.py:277
  1559.5 69.1 %reduce-scatter.27.cloned.1.call-done = f32[512,704]{0,1:T(8,128)} async-done(((f32[2048,704]{0,1:T(8,128)}), f32[512,704]{0,1:T(8,128)}) %reduce-scatter.27.cloned.1.call-update) | async-done | bytes 1441808 | tf_op jit(solution)/shard_map/reduce_scatter | solution.py:278
  1628.7 38.8 %reduce-scatter.17.cloned.1.call-done = f32[512,256]{1,0:T(8,128)} async-done(((f32[2048,256]{1,0:T(8,128)}), f32[512,256]{1,0:T(8,128)}) %reduce-scatter.17.cloned.1.call-update) | async-done | bytes 524304 | tf_op jit(solution)/shard_map/reduce_scatter | solution.py:272
  1667.4 38.6 %reduce-scatter.23.cloned.1.call-done = f32[256,512]{1,0:T(8,128)} async-done(((f32[256,2048]{1,0:T(8,128)}), f32[256,512]{1,0:T(8,128)}) %reduce-scatter.23.cloned.1.call-update) | async-done | bytes 524304 | tf_op jit(solution)/shard_map/reduce_scatter | solution.py:275
  1706.0 59.0 %all-reduce.7.cloned.1.call-done = (f32[512,128]{1,0:T(8,128)}, f32[512,128]{1,0:T(8,128)}) async-done(((f32[512,128]{1,0:T(8,128)}, f32[512,128]{1,0:T(8,128)}), (f32[512,128]{1,0:T(8,128)}, f32[512,128]{1,0:T(8,128)})) %all-reduce.7.cloned.1.call-update) | async-done | bytes 524304 | tf_op jit(solution)/shard_map/psum | solution.py:281
  (345 shorter events, 246.1 us)
Async XLA Ops:
  7.2 32.3 %all-gather.17.cloned.1.call-start = ((), (), s32[]{:S(2)}) async-start(), calls=%async_computation.13 | async-start | bytes 1310720 | tf_op jit(solution)/shard_map/all_gather | solution.py:160
  9.0 115.2 %all-gather.13.cloned.1.call-start = ((), (), s32[]{:S(2)}) async-start(), calls=%async_computation.11 | async-start | bytes 9437184 | tf_op jit(solution)/shard_map/all_gather | solution.py:178
  20.9 275.0 %copy-start.2 = (bf16[256,2048]{0,1:T(8,128)(2,1)}, bf16[256,2048]{0,1:T(8,128)(2,1)S(1)}, u32[]{:S(2)}) copy-start(bf16[256,2048]{0,1:T(8,128)(2,1)S(1)} %copy.114) | copy-start | bytes 3145732
  21.2 18.3 %copy-start.26 = (f32[512,704]{0,1:T(8,128)S(1)}, f32[512,704]{0,1:T(8,128)}, u32[]{:S(2)}) copy-start(f32[512,704]{0,1:T(8,128)} %param.29) | copy-start | bytes 4325380
  23.2 128.1 %all-gather.15.cloned.1.call-start = ((), (), s32[]{:S(2)}) async-start(), calls=%async_computation.12 | async-start | bytes 1310720 | tf_op jit(solution)/shard_map/all_gather | solution.py:157
  24.0 252.7 %all-gather.19.cloned.1.call-start = ((), (), s32[]{:S(2)}) async-start(), calls=%async_computation.14 | async-start | bytes 9437184 | tf_op jit(solution)/shard_map/all_gather | solution.py:197
  39.5 271.1 %all-gather.23.cloned.1.call-start = ((), (), s32[]{:S(2)}) async-start(), calls=%async_computation.16 | async-start | bytes 3604480 | tf_op jit(solution)/shard_map/all_gather | solution.py:162
  40.6 93.5 %copy-start.52 = (f32[64]{0:T(128)}, f32[64]{0:T(128)S(1)}, u32[]{:S(2)}) copy-start(f32[64]{0:T(128)S(1)} %multiply_power_fusion) | copy-start | bytes 772
  48.9 124.8 %copy-start.36 = (s32[2048]{0:T(1024)}, s32[2048]{0:T(1024)S(1)}, u32[]{:S(2)}) copy-start(s32[2048]{0:T(1024)S(1)} %fusion.85) | copy-start | bytes 24580
  49.1 194.8 %copy-start.38 = (s32[2048]{0:T(1024)}, s32[2048]{0:T(1024)S(1)}, u32[]{:S(2)}) copy-start(s32[2048]{0:T(1024)S(1)} %get-tuple-element.398) | copy-start | bytes 24580
  60.9 68.0 %copy-start.43 = (s32[2048]{0:T(1024)}, s32[2048]{0:T(1024)S(1)}, u32[]{:S(2)}) copy-start(s32[2048]{0:T(1024)S(1)} %gather_fusion) | copy-start | bytes 24580
  71.1 53.1 %copy-start.25 = (bf16[2048,128]{1,0:T(8,128)(2,1)}, bf16[2048,128]{1,0:T(8,128)(2,1)S(1)}, u32[]{:S(2)}) copy-start(bf16[2048,128]{1,0:T(8,128)(2,1)S(1)} %all_gather.46) | copy-start | bytes 1572868
  80.6 48.6 %copy-start.21 = (bf16[2048,128]{1,0:T(8,128)(2,1)}, bf16[2048,128]{1,0:T(8,128)(2,1)S(1)}, u32[]{:S(2)}) copy-start(bf16[2048,128]{1,0:T(8,128)(2,1)S(1)} %all_gather.45) | copy-start | bytes 1572868
  239.8 21.7 %copy-start.4 = (bf16[2048,128]{1,0:T(8,128)(2,1)}, bf16[2048,128]{1,0:T(8,128)(2,1)S(1)}, u32[]{:S(2)}) copy-start(bf16[2048,128]{1,0:T(8,128)(2,1)S(1)} %get-tuple-element.636) | copy-start | bytes 1572868
  239.8 21.7 %copy-start.6 = (bf16[2048,128]{1,0:T(8,128)(2,1)}, bf16[2048,128]{1,0:T(8,128)(2,1)S(1)}, u32[]{:S(2)}) copy-start(bf16[2048,128]{1,0:T(8,128)(2,1)S(1)} %get-tuple-element.637) | copy-start | bytes 1572868
  239.8 21.7 %copy-start.11 = (bf16[4,512,2,128]{3,1,2,0:T(8,128)(2,1)}, bf16[4,512,2,128]{3,1,2,0:T(8,128)(2,1)S(1)}, u32[]{:S(2)}) copy-start(bf16[4,512,2,128]{3,1,2,0:T(8,128)(2,1)S(1)} %get-tuple-element.645) | copy-start | bytes 3145732
  263.8 31.2 %all-to-all-start = ((bf16[8,256,256]{1,2,0:T(8,128)(2,1)}), bf16[8,256,256]{1,2,0:T(8,128)(2,1)S(1)}, u32[]{:S(2)}, u32[]{:S(2)}) async-start(bf16[8,256,256]{1,2,0:T(8,128)(2,1)} %copy.124), calls=%async_computation | async-start | bytes 2097152 | tf_op jit(solution)/shard_map/all_to_all | solution.py:198
  268.4 116.9 %all-gather.21.cloned.1.call-start = ((), (), s32[]{:S(2)}) async-start(), calls=%async_computation.15 | async-start | bytes 9437184 | tf_op jit(solution)/shard_map/all_gather | solution.py:202
  276.7 487.3 %copy-start.34 = (f32[4,1,512]{2,1,0:T(1,128)}, f32[4,1,512]{2,1,0:T(1,128)S(1)}, u32[]{:S(2)}) copy-start(f32[4,1,512]{2,1,0:T(1,128)S(1)} %convert_element_type.144) | copy-start | bytes 24580
  303.0 460.9 %copy-start = (f32[256,2048]{0,1:T(8,128)}, f32[256,2048]{0,1:T(8,128)S(1)}, u32[]{:S(2)}) copy-start(f32[256,2048]{0,1:T(8,128)S(1)} %get-tuple-element.395) | copy-start | bytes 6291460
  303.1 460.9 %copy-start.45 = (f32[256]{0:T(256)}, f32[256]{0:T(256)S(1)}, u32[]{:S(2)}) copy-start(f32[256]{0:T(256)S(1)} %add_rsqrt_fusion) | copy-start | bytes 3076
  304.7 122.8 %all-gather.25.cloned.1.call-start = ((), (), s32[]{:S(2)}) async-start(), calls=%async_computation.17 | async-start | bytes 3604480 | tf_op jit(solution)/shard_map/all_gather | solution.py:163
  307.1 163.8 %all-gather.27.cloned.1.call-start = ((), (), s32[]{:S(2)}) async-start(), calls=%async_computation.18 | async-start | bytes 3604480 | tf_op jit(solution)/shard_map/all_gather | solution.py:164
  309.8 244.7 %all-gather.29.cloned.1.call-start = ((), (), s32[]{:S(2)}) async-start(), calls=%async_computation.20 | async-start | bytes 9437184 | tf_op jit(solution)/shard_map/all_gather | solution.py:179
  310.6 450.3 %reduce-scatter.13.cloned.1.call-start = ((), (), s32[]{:S(2)}) async-start(), calls=%async_computation.21 | async-start | bytes 18874368 | tf_op jit(solution)/shard_map/reduce_scatter | solution.py:222
  594.1 252.7 %all-gather.31.cloned.1.call-start = ((), (), s32[]{:S(2)}) async-start(), calls=%async_computation.22 | async-start | bytes 9437184 | tf_op jit(solution)/shard_map/all_gather | solution.py:232
  595.7 170.0 %copy-start.14 = (bf16[256,2048]{0,1:T(8,128)(2,1)}, bf16[256,2048]{0,1:T(8,128)(2,1)S(1)}, u32[]{:S(2)}) copy-start(bf16[256,2048]{0,1:T(8,128)(2,1)S(1)} %copy.127) | copy-start | bytes 3145732
  765.7 426.4 %reduce-scatter.15.cloned.1.call-start = ((), (), s32[]{:S(2)}) async-start(), calls=%async_computation.23 | async-start | bytes 21233664 | tf_op jit(solution)/shard_map/reduce_scatter | solution.py:252
  765.8 92.1 %copy-start.37 = (s32[2048]{0:T(1024)S(1)}, s32[2048]{0:T(1024)}, u32[]{:S(2)}) copy-start(s32[2048]{0:T(1024)} %copy-done.36) | copy-start | bytes 24580
  853.9 19.1 %copy-start.5 = (bf16[2048,128]{1,0:T(8,128)(2,1)S(1)}, bf16[2048,128]{1,0:T(8,128)(2,1)}, u32[]{:S(2)}) copy-start(bf16[2048,128]{1,0:T(8,128)(2,1)} %copy-done.4) | copy-start | bytes 1572868
  853.9 19.1 %copy-start.7 = (bf16[2048,128]{1,0:T(8,128)(2,1)S(1)}, bf16[2048,128]{1,0:T(8,128)(2,1)}, u32[]{:S(2)}) copy-start(bf16[2048,128]{1,0:T(8,128)(2,1)} %copy-done.6) | copy-start | bytes 1572868
  853.9 19.1 %copy-start.12 = (bf16[4,512,2,128]{3,1,2,0:T(8,128)(2,1)S(1)}, bf16[4,512,2,128]{3,1,2,0:T(8,128)(2,1)}, u32[]{:S(2)}) copy-start(bf16[4,512,2,128]{3,1,2,0:T(8,128)(2,1)} %copy-done.11) | copy-start | bytes 3145732
  1005.9 187.3 %copy-start.53 = (f32[64]{0:T(128)S(1)}, f32[64]{0:T(128)}, u32[]{:S(2)}) copy-start(f32[64]{0:T(128)} %copy-done.52) | copy-start | bytes 772
  1005.9 187.6 %copy-start.10 = (bf16[256,2048]{0,1:T(8,128)(2,1)S(1)}, bf16[256,2048]{0,1:T(8,128)(2,1)}, u32[]{:S(2)}) copy-start(bf16[256,2048]{0,1:T(8,128)(2,1)} %fusion.50) | copy-start | bytes 3145732
  1005.9 261.8 %reduce-scatter.19.cloned.1.call-start = ((), (), s32[]{:S(2)}) async-start(), calls=%async_computation.25 | async-start | bytes 1310720 | tf_op jit(solution)/shard_map/reduce_scatter | solution.py:273
  1194.9 72.7 %reduce-scatter.21.cloned.1.call-start = ((), (), s32[]{:S(2)}) async-start(), calls=%async_computation.26 | async-start | bytes 1310720 | tf_op jit(solution)/shard_map/reduce_scatter | solution.py:274
  1196.4 226.1 %reduce-scatter.11.cloned.1.call-start = ((), (), s32[]{:S(2)}) async-start(), calls=%async_computation.19 | async-start | bytes 18874368 | tf_op jit(solution)/shard_map/reduce_scatter | solution.py:208
  1209.2 281.2 %reduce-scatter.29.cloned.1.call-start = ((), (), s32[]{:S(2)}) async-start(), calls=%async_computation.30 | async-start | bytes 7208960 | tf_op jit(solution)/shard_map/reduce_scatter | solution.py:279
  1220.4 339.1 %reduce-scatter.25.cloned.1.call-start = ((), (), s32[]{:S(2)}) async-start(), calls=%async_computation.28 | async-start | bytes 7208960 | tf_op jit(solution)/shard_map/reduce_scatter | solution.py:277
  1231.7 396.9 %reduce-scatter.27.cloned.1.call-start = ((), (), s32[]{:S(2)}) async-start(), calls=%async_computation.29 | async-start | bytes 7208960 | tf_op jit(solution)/shard_map/reduce_scatter | solution.py:278
  1243.0 424.5 %reduce-scatter.17.cloned.1.call-start = ((), (), s32[]{:S(2)}) async-start(), calls=%async_computation.24 | async-start | bytes 2621440 | tf_op jit(solution)/shard_map/reduce_scatter | solution.py:272
  1250.5 455.5 %reduce-scatter.23.cloned.1.call-start = ((), (), s32[]{:S(2)}) async-start(), calls=%async_computation.27 | async-start | bytes 2621440 | tf_op jit(solution)/shard_map/reduce_scatter | solution.py:275
  1260.1 505.0 %all-reduce.7.cloned.1.call-start = ((), (), s32[]{:S(2)}) async-start(), calls=%async_computation.31 | async-start | bytes 1048576 | tf_op jit(solution)/shard_map/psum | solution.py:281
  1264.3 158.3 %copy-start.1 = (f32[256,2048]{0,1:T(8,128)S(1)}, f32[256,2048]{0,1:T(8,128)}, u32[]{:S(2)}) copy-start(f32[256,2048]{0,1:T(8,128)} %copy-done) | copy-start | bytes 6291460
  1264.3 158.2 %copy-start.35 = (f32[4,1,512]{2,1,0:T(1,128)S(1)}, f32[4,1,512]{2,1,0:T(1,128)}, u32[]{:S(2)}) copy-start(f32[4,1,512]{2,1,0:T(1,128)} %copy-done.34) | copy-start | bytes 24580
  1264.3 158.2 %copy-start.46 = (f32[256]{0:T(256)S(1)}, f32[256]{0:T(256)}, u32[]{:S(2)}) copy-start(f32[256]{0:T(256)} %copy-done.45) | copy-start | bytes 3076
  1264.3 158.2 %copy-start.50 = (f32[256]{0:T(256)S(1)}, f32[256]{0:T(256)}, u32[]{:S(2)}) copy-start(f32[256]{0:T(256)} %copy-done.49) | copy-start | bytes 3076
  1427.5 20.2 %copy-start.20 = (bf16[256,2048]{0,1:T(8,128)(2,1)S(1)}, bf16[256,2048]{0,1:T(8,128)(2,1)}, u32[]{:S(2)}) copy-start(bf16[256,2048]{0,1:T(8,128)(2,1)} %get-tuple-element.384) | copy-start | bytes 3145732
  (41 other events, 227.1 us)
Sparse Core Ops, SparseCore 0:
  10.4 29.0 all-gather.16
  41.7 82.4 all-gather.12
  126.6 24.6 all-gather.14
  152.8 82.0 all-gather.18
  236.5 40.0 all-gather.22
  304.8 80.4 all-gather.20
  387.7 39.7 all-gather.24
  429.3 41.5 all-gather.26
  472.4 82.0 all-gather.28
  594.2 166.6 reduce-scatter.12
  765.8 80.9 all-gather.30
  1006.0 186.0 reduce-scatter.14
  1195.0 26.3 reduce-scatter.18
  1224.2 27.9 reduce-scatter.20
  1254.4 168.1 reduce-scatter.10
  1426.0 64.4 reduce-scatter.28
  1493.8 65.6 reduce-scatter.24
  1563.0 65.6 reduce-scatter.26
  1632.2 35.1 reduce-scatter.16
  1670.8 35.1 reduce-scatter.22
  1708.4 56.5 all-reduce.6
where the time goes:
time: 1780 us
  waiting for transfers between devices  1180 us (66%)
  matrix products  230 us (13%)
  local copies, waits for them, and re-layouts  159 us (9%)
  other arithmetic  96.3 us (5%)
  blocking collectives  68.7 us (4%)
    reduce_scatter x1, waiting for transfers between devices, local(): lax.psum_scatter(grad_parts, 'col', scatter_dimension=0, tiled=True)  184 us
    reduce_scatter x1, waiting for transfers between devices, local(): lax.psum_scatter(jnp.dot(gate_grad, gate_copy.T, preferred_element_type=j...  165 us
    reduce_scatter x1, waiting for transfers between devices, local(): lax.psum_scatter(jnp.dot(hidden, down_copy, preferred_element_type=jnp.fl...  155 us
    all_gather x1, waiting for transfers between devices, local(): lax.all_gather(out_grad, 'col', axis=0, tiled=True)  83.7 us
    all_gather x1, waiting for transfers between devices, local(): middle_rows = lax.all_gather(middle_low, 'col', axis=0, tiled=True)  81 us
    all_gather x1, waiting for transfers between devices, local(): lax.all_gather(normed_two.astype(jnp.bfloat16), 'col', axis=0, tiled=True)  74.6 us
    reduce_scatter x1, waiting for transfers between devices, local(): lax.psum_scatter(up_wgrad, 'row', scatter_dimension=0, tiled=True)  69.1 us
    reduce_scatter x1, waiting for transfers between devices, local(): lax.psum_scatter(gate_wgrad, 'row', scatter_dimension=0, tiled=True)  69.1 us
  transfers between devices with their start and end apart: 22, of which 18 were waited for; matrix products, arithmetic and copies ran while one was open for 16% of the time, Pallas kernels for 0%

commit v1 on v0

--- a/solution.py
+++ b/solution.py
@@ -6,6 +6,26 @@
 norm_eps = 1e-05
 rope_base = 10000.0
 masked_score = -1e30
+
+
+def lift_tracks_by_axis(block_here, lane_axis):
+    num_devices = lax.psum(1, lane_axis)
+    kept_arr = range(num_devices)
+    extra = map(lambda w: (w, (w + 1) % num_devices), kept_arr)
+    steps_seen = list(extra)
+    q_next = range(num_devices)
+    row_out = map(lambda w: (w, (w - 1) % num_devices), q_next)
+    pile = list(row_out)
+    last, y_new = ([block_here], [block_here])
+    for _ in range(num_devices // 2):
+        local_now = lax.ppermute(last[-1], lane_axis, steps_seen)
+        last.append(local_now)
+    for _ in range((num_devices - 1) // 2):
+        taken_in = lax.ppermute(y_new[-1], lane_axis, pile)
+        y_new.append(taken_in)
+    arr_next = jnp.concatenate([*last[::-1], *y_new[1:]], axis=0)
+    val2 = lax.axis_index(lane_axis)
+    return jnp.roll(arr_next, (val2 - num_devices // 2) * block_here.shape[0], axis=0)
 
 
 def rotate_pairs(values, positions, direction):
@@ -229,7 +249,7 @@
     middle_part, gain_two_grad = norm_backward(middle, factor_two, gain_two, normed_two_grad)
     middle_grad = out_grad.astype(jnp.float32) + middle_part
     middle_low = middle_grad.astype(jnp.bfloat16)
-    middle_rows = lax.all_gather(middle_low, "col", axis=0, tiled=True)
+    middle_rows = lift_tracks_by_axis(middle_low, "col")
     mixed_grad_slot = jnp.dot(middle_rows, out_copy.T, preferred_element_type=jnp.float32).astype(
         jnp.bfloat16
     )

time: 1780 us -> 1800 us (1.011)
    all_gather x1 -> x0, waiting for transfers between devices: 81 us -> none  [local(): middle_rows = lax.all_gather(middle_low, 'col', axis=0, tiled=True)]
    ppermute x0 -> x7, waiting for transfers between devices: none -> 77.7 us  [the longest x4 77.6 us: lift_tracks_by_axis(): local_now = lax.ppermute(last[-1], lane_axis, steps_seen)]
    unnamed x133 -> x160, local copies, waits for them, and re-layouts: 23.7 us -> 36.3 us
  transfers between devices with their start and end apart: 22 -> 28, of which waited for: 18 -> 22; matrix products, arithmetic and copies ran while one was open for 16% -> 16% of each run, Pallas kernels for 0% -> 0%
where the time goes in v1:
time: 1800 us; the launch traced here: 1790 us
  waiting for transfers between devices  1180 us (66%)
  matrix products  226 us (13%)
  local copies, waits for them, and re-layouts  172 us (10%)
  other arithmetic  95.6 us (5%)
  blocking collectives  68.6 us (4%)
    reduce_scatter x1, waiting for transfers between devices, local(): lax.psum_scatter(grad_parts, 'col', scatter_dimension=0, tiled=True)  184 us
    reduce_scatter x1, waiting for transfers between devices, local(): lax.psum_scatter(jnp.dot(gate_grad, gate_copy.T, preferred_element_type=j...  165 us
    reduce_scatter x1, waiting for transfers between devices, local(): lax.psum_scatter(jnp.dot(hidden, down_copy, preferred_element_type=jnp.fl...  155 us
    all_gather x1, waiting for transfers between devices, local(): lax.all_gather(out_grad, 'col', axis=0, tiled=True)  83.7 us
    ppermute x4, waiting for transfers between devices, lift_tracks_by_axis(): local_now = lax.ppermute(last[-1], lane_axis, steps_seen)  77.6 us
    all_gather x1, waiting for transfers between devices, local(): lax.all_gather(normed_two.astype(jnp.bfloat16), 'col', axis=0, tiled=True)  74.5 us
    reduce_scatter x1, waiting for transfers between devices, local(): lax.psum_scatter(gate_wgrad, 'row', scatter_dimension=0, tiled=True)  69.1 us
    reduce_scatter x1, waiting for transfers between devices, local(): lax.psum_scatter(up_wgrad, 'row', scatter_dimension=0, tiled=True)  69.1 us
  transfers between devices with their start and end apart: 28, of which 22 were waited for; matrix products, arithmetic and copies ran while one was open for 16% of the time, Pallas kernels for 0%

profile of v1, /device:TPU:0, one launch (start us, length us, event | category | flops | bytes accessed | tf_op | source)
XLA Modules:
  0.0 1791.2 jit_solution(1505286798181201733)
XLA Ops:
  9.8 9.6 all-gather
  24.1 15.4 all-gather.16.cloned.1.call-done
  40.9 8.0 scatter_custom_fusion
  49.1 11.8 gather_fusion
  61.0 10.1 all_gather.43
  71.1 9.6 all_gather.42
  86.5 37.7 %all-gather.12.cloned.1.call-done = bf16[2048,2048]{0,1:T(8,128)(2,1)} async-done(((bf16[256,2048]{0,1:T(8,128)(2,1)}), bf16[2048,2048]{0,1:T(8,128)(2,1)}) %all-gather.12.cloned.1.call-update) | async-done | bytes 8388624 | tf_op jit(solution)/shard_map/all_gather | solution.py:198
  173.7 13.9 gather_fusion.1
  189.1 50.7 %while.27 = (s32[]{:T(128)}, bf16[4,512,2,128]{3,1,0,2:T(8,128)(2,1)}, f32[4,2,512]{2,1,0:T(2,128)S(1)}, s32[4]{0:T(128)S(1)}, s32[2048]{0:T(1024)S(1)}, /*index...) while((s32[]{:T(128)}, ...), condition=%wide.region_8.9_spmd, body=%wide.region_5.8_spmd.sunk | while | flops 1102183936 | bytes 30984376 | solution.py:100
  243.8 15.1 gather_fusion.4
  268.4 8.2 all-gather.1
  276.7 18.3 %all-to-all-done = bf16[8,256,256]{1,2,0:T(8,128)(2,1)S(1)} async-done(((bf16[8,256,256]{1,2,0:T(8,128)(2,1)}), bf16[8,256,256]{1,2,0:T(8,128)(2,1)S(1)}, u32[]{:S(2)}, u32[]{:S(2)}) %all-to-all-start) | async-done | bytes 1048608 | tf_op jit(solution)/shard_map/all_to_all | solution.py:218
  310.9 74.5 %all-gather.20.cloned.1.call-done = bf16[2048,2048]{0,1:T(8,128)(2,1)} async-done(((bf16[256,2048]{0,1:T(8,128)(2,1)}), bf16[2048,2048]{0,1:T(8,128)(2,1)}) %all-gather.20.cloned.1.call-update) | async-done | bytes 8388624 | tf_op jit(solution)/shard_map/all_gather | solution.py:222
  385.4 11.1 fusion.107
  396.5 31.1 %all-gather.24.cloned.1.call-done = bf16[2048,704]{0,1:T(8,128)(2,1)} async-done(((bf16[512,704]{0,1:T(8,128)(2,1)}), bf16[2048,704]{0,1:T(8,128)(2,1)}) %all-gather.24.cloned.1.call-update) | async-done | bytes 2883600 | tf_op jit(solution)/shard_map/all_gather | solution.py:183
  427.6 11.1 fusion.108
  438.6 32.3 %all-gather.26.cloned.1.call-done = bf16[704,2048]{1,0:T(8,128)(2,1)} async-done(((bf16[704,512]{1,0:T(8,128)(2,1)}), bf16[704,2048]{1,0:T(8,128)(2,1)}) %all-gather.26.cloned.1.call-update) | async-done | bytes 2883600 | tf_op jit(solution)/shard_map/all_gather | solution.py:184
  471.0 83.7 %all-gather.28.cloned.1.call-done = bf16[2048,2048]{1,0:T(8,128)(2,1)} async-done(((bf16[256,2048]{1,0:T(8,128)(2,1)}), bf16[2048,2048]{1,0:T(8,128)(2,1)}) %all-gather.28.cloned.1.call-update) | async-done | bytes 8388624 | tf_op jit(solution)/shard_map/all_gather | solution.py:199
  554.6 15.3 multiply_convert_fusion
  569.9 10.4 fusion.103
  580.4 13.9 convolution_add_fusion
  595.8 165.3 %reduce-scatter.13.cloned.1.call-done = f32[256,2048]{0,1:T(8,128)} async-done(((f32[2048,2048]{0,1:T(8,128)}), f32[256,2048]{0,1:T(8,128)}) %reduce-scatter.13.cloned.1.call-update) | async-done | bytes 2097168 | tf_op jit(solution)/shard_map/reduce_scatter | solution.py:242
  764.9 16.0 collective-permute-done
  784.5 21.4 %collective-permute-done.1 = bf16[256,2048]{0,1:T(8,128)(2,1)S(1)} collective-permute-done((bf16[256,2048]{0,1:T(8,128)(2,1)S(1)}, bf16[256,2048]{0,1:T(8,128)(2,1)S(1)}, u32[]{:S(2)}, u32[]{:S(2)}) %collective-permute-start.1) | collective-permute-done | bytes 1048608 | tf_op jit(solution)/shard_map/ppermute | solution.py:21
  809.5 20.2 %collective-permute-done.2 = bf16[256,2048]{0,1:T(8,128)(2,1)} collective-permute-done((bf16[256,2048]{0,1:T(8,128)(2,1)S(1)}, bf16[256,2048]{0,1:T(8,128)(2,1)}, u32[]{:S(2)}, u32[]{:S(2)}) %collective-permute-start.2) | collective-permute-done | bytes 1048608 | tf_op jit(solution)/shard_map/ppermute | solution.py:21
  833.6 20.0 %collective-permute-done.3 = bf16[256,2048]{0,1:T(8,128)(2,1)} collective-permute-done((bf16[256,2048]{0,1:T(8,128)(2,1)}, bf16[256,2048]{0,1:T(8,128)(2,1)}, u32[]{:S(2)}, u32[]{:S(2)}) %collective-permute-start.3) | collective-permute-done | bytes 1048608 | tf_op jit(solution)/shard_map/ppermute | solution.py:21
  873.5 15.0 gather_fusion.5
  888.5 77.5 %while.28 = (s32[]{:T(128)}, f32[2048,128]{1,0:T(8,128)S(1)}, f32[2048,128]{1,0:T(8,128)}, f32[4,512,2,128]{3,1,0,2:T(8,128)}, s32[4]{0:T(128)S(1)}, /*index=5*/...) while((s32[]{:T(128)}, f32[2048,128]{1,0:T(8,128)S(1)}, ...), condition=%wide.region_15.16_spmd.clone, body=%wide.region_13.15_spmd.clone.sunk | while | flops 2720398848 | bytes 83409176 | solution.py:139
  970.9 14.6 gather_fusion.6
  986.9 8.6 gather_fusion.7
  998.5 9.0 subtract_convert_fusion
  1012.8 8.8 pad_maximum_fusion
  1023.4 184.4 %reduce-scatter.15.cloned.1.call-done = f32[256,2304]{0,1:T(8,128)} async-done(((f32[2048,2304]{0,1:T(8,128)}), f32[256,2304]{0,1:T(8,128)}) %reduce-scatter.15.cloned.1.call-update) | async-done | bytes 2359312 | tf_op jit(solution)/shard_map/reduce_scatter | solution.py:272
  1212.1 12.7 fusion.102
  1224.9 11.1 fusion.106
  1236.1 11.2 fusion.104
  1247.4 11.1 fusion.105
  1258.8 7.2 fusion.66
  1268.1 7.5 fusion.47
  1283.1 155.2 %reduce-scatter.11.cloned.1.call-done = f32[256,2048]{0,1:T(8,128)} async-done(((f32[2048,2048]{0,1:T(8,128)}), f32[256,2048]{0,1:T(8,128)}) %reduce-scatter.11.cloned.1.call-update) | async-done | bytes 2097168 | tf_op jit(solution)/shard_map/reduce_scatter | solution.py:228
  1443.3 17.1 all-reduce.4
  1464.9 14.1 all-reduce.2
  1479.0 27.2 %reduce-scatter.29.cloned.1.call-done = f32[704,512]{1,0:T(8,128)} async-done(((f32[704,2048]{1,0:T(8,128)}), f32[704,512]{1,0:T(8,128)}) %reduce-scatter.29.cloned.1.call-update) | async-done | bytes 1441808 | tf_op jit(solution)/shard_map/reduce_scatter | solution.py:299
  1506.3 69.1 %reduce-scatter.25.cloned.1.call-done = f32[512,704]{0,1:T(8,128)} async-done(((f32[2048,704]{0,1:T(8,128)}), f32[512,704]{0,1:T(8,128)}) %reduce-scatter.25.cloned.1.call-update) | async-done | bytes 1441808 | tf_op jit(solution)/shard_map/reduce_scatter | solution.py:297
  1575.4 69.1 %reduce-scatter.27.cloned.1.call-done = f32[512,704]{0,1:T(8,128)} async-done(((f32[2048,704]{0,1:T(8,128)}), f32[512,704]{0,1:T(8,128)}) %reduce-scatter.27.cloned.1.call-update) | async-done | bytes 1441808 | tf_op jit(solution)/shard_map/reduce_scatter | solution.py:298
  1644.5 38.6 %reduce-scatter.17.cloned.1.call-done = f32[512,256]{1,0:T(8,128)} async-done(((f32[2048,256]{1,0:T(8,128)}), f32[512,256]{1,0:T(8,128)}) %reduce-scatter.17.cloned.1.call-update) | async-done | bytes 524304 | tf_op jit(solution)/shard_map/reduce_scatter | solution.py:292
  1683.1 38.8 %reduce-scatter.23.cloned.1.call-done = f32[256,512]{1,0:T(8,128)} async-done(((f32[256,2048]{1,0:T(8,128)}), f32[256,512]{1,0:T(8,128)}) %reduce-scatter.23.cloned.1.call-update) | async-done | bytes 524304 | tf_op jit(solution)/shard_map/reduce_scatter | solution.py:295
  1721.9 58.9 %all-reduce.7.cloned.1.call-done = (f32[512,128]{1,0:T(8,128)}, f32[512,128]{1,0:T(8,128)}) async-done(((f32[512,128]{1,0:T(8,128)}, f32[512,128]{1,0:T(8,128)}), (f32[512,128]{1,0:T(8,128)}, f32[512,128]{1,0:T(8,128)})) %all-reduce.7.cloned.1.call-update) | async-done | bytes 524304 | tf_op jit(solution)/shard_map/psum | solution.py:301
  (384 shorter events, 285.4 us)
Async XLA Ops:
  7.2 32.3 %all-gather.16.cloned.1.call-start = ((), (), s32[]{:S(2)}) async-start(), calls=%async_computation.13 | async-start | bytes 1310720 | tf_op jit(solution)/shard_map/all_gather | solution.py:180
  9.1 115.1 %all-gather.12.cloned.1.call-start = ((), (), s32[]{:S(2)}) async-start(), calls=%async_computation.11 | async-start | bytes 9437184 | tf_op jit(solution)/shard_map/all_gather | solution.py:198
  21.0 274.9 %copy-start.2 = (bf16[256,2048]{0,1:T(8,128)(2,1)}, bf16[256,2048]{0,1:T(8,128)(2,1)S(1)}, u32[]{:S(2)}) copy-start(bf16[256,2048]{0,1:T(8,128)(2,1)S(1)} %copy.114) | copy-start | bytes 3145732
  23.3 128.0 %all-gather.14.cloned.1.call-start = ((), (), s32[]{:S(2)}) async-start(), calls=%async_computation.12 | async-start | bytes 1310720 | tf_op jit(solution)/shard_map/all_gather | solution.py:177
  24.1 252.6 %all-gather.18.cloned.1.call-start = ((), (), s32[]{:S(2)}) async-start(), calls=%async_computation.14 | async-start | bytes 9437184 | tf_op jit(solution)/shard_map/all_gather | solution.py:217
  39.6 271.3 %all-gather.22.cloned.1.call-start = ((), (), s32[]{:S(2)}) async-start(), calls=%async_computation.16 | async-start | bytes 3604480 | tf_op jit(solution)/shard_map/all_gather | solution.py:182
  40.6 93.5 %copy-start.58 = (f32[64]{0:T(128)}, f32[64]{0:T(128)S(1)}, u32[]{:S(2)}) copy-start(f32[64]{0:T(128)S(1)} %multiply_power_fusion) | copy-start | bytes 772
  48.9 124.8 %copy-start.41 = (s32[2048]{0:T(1024)}, s32[2048]{0:T(1024)S(1)}, u32[]{:S(2)}) copy-start(s32[2048]{0:T(1024)S(1)} %fusion.92) | copy-start | bytes 24580
  49.1 194.7 %copy-start.43 = (s32[2048]{0:T(1024)}, s32[2048]{0:T(1024)S(1)}, u32[]{:S(2)}) copy-start(s32[2048]{0:T(1024)S(1)} %get-tuple-element.398) | copy-start | bytes 24580
  60.9 68.0 %copy-start.49 = (s32[2048]{0:T(1024)}, s32[2048]{0:T(1024)S(1)}, u32[]{:S(2)}) copy-start(s32[2048]{0:T(1024)S(1)} %gather_fusion) | copy-start | bytes 24580
  71.1 53.1 %copy-start.29 = (bf16[2048,128]{1,0:T(8,128)(2,1)}, bf16[2048,128]{1,0:T(8,128)(2,1)S(1)}, u32[]{:S(2)}) copy-start(bf16[2048,128]{1,0:T(8,128)(2,1)S(1)} %all_gather.43) | copy-start | bytes 1572868
  80.6 48.6 %copy-start.25 = (bf16[2048,128]{1,0:T(8,128)(2,1)}, bf16[2048,128]{1,0:T(8,128)(2,1)S(1)}, u32[]{:S(2)}) copy-start(bf16[2048,128]{1,0:T(8,128)(2,1)S(1)} %all_gather.42) | copy-start | bytes 1572868
  263.7 31.2 %all-to-all-start = ((bf16[8,256,256]{1,2,0:T(8,128)(2,1)}), bf16[8,256,256]{1,2,0:T(8,128)(2,1)S(1)}, u32[]{:S(2)}, u32[]{:S(2)}) async-start(bf16[8,256,256]{1,2,0:T(8,128)(2,1)} %copy.124), calls=%async_computation | async-start | bytes 2097152 | tf_op jit(solution)/shard_map/all_to_all | solution.py:218
  268.4 117.0 %all-gather.20.cloned.1.call-start = ((), (), s32[]{:S(2)}) async-start(), calls=%async_computation.15 | async-start | bytes 9437184 | tf_op jit(solution)/shard_map/all_gather | solution.py:222
  276.6 487.5 %copy-start.39 = (f32[4,1,512]{2,1,0:T(1,128)}, f32[4,1,512]{2,1,0:T(1,128)S(1)}, u32[]{:S(2)}) copy-start(f32[4,1,512]{2,1,0:T(1,128)S(1)} %convert_element_type.144) | copy-start | bytes 24580
  303.0 461.1 %copy-start = (f32[256,2048]{0,1:T(8,128)}, f32[256,2048]{0,1:T(8,128)S(1)}, u32[]{:S(2)}) copy-start(f32[256,2048]{0,1:T(8,128)S(1)} %get-tuple-element.395) | copy-start | bytes 6291460
  303.0 461.1 %copy-start.51 = (f32[256]{0:T(256)}, f32[256]{0:T(256)S(1)}, u32[]{:S(2)}) copy-start(f32[256]{0:T(256)S(1)} %add_rsqrt_fusion) | copy-start | bytes 3076
  304.8 122.8 %all-gather.24.cloned.1.call-start = ((), (), s32[]{:S(2)}) async-start(), calls=%async_computation.17 | async-start | bytes 3604480 | tf_op jit(solution)/shard_map/all_gather | solution.py:183
  307.2 163.8 %all-gather.26.cloned.1.call-start = ((), (), s32[]{:S(2)}) async-start(), calls=%async_computation.18 | async-start | bytes 3604480 | tf_op jit(solution)/shard_map/all_gather | solution.py:184
  310.0 244.6 %all-gather.28.cloned.1.call-start = ((), (), s32[]{:S(2)}) async-start(), calls=%async_computation.20 | async-start | bytes 9437184 | tf_op jit(solution)/shard_map/all_gather | solution.py:199
  310.8 450.3 %reduce-scatter.13.cloned.1.call-start = ((), (), s32[]{:S(2)}) async-start(), calls=%async_computation.21 | async-start | bytes 18874368 | tf_op jit(solution)/shard_map/reduce_scatter | solution.py:242
  594.3 613.5 %reduce-scatter.15.cloned.1.call-start = ((), (), s32[]{:S(2)}) async-start(), calls=%async_computation.22 | async-start | bytes 21233664 | tf_op jit(solution)/shard_map/reduce_scatter | solution.py:272
  595.8 169.0 %copy-start.14 = (bf16[256,2048]{0,1:T(8,128)(2,1)}, bf16[256,2048]{0,1:T(8,128)(2,1)S(1)}, u32[]{:S(2)}) copy-start(bf16[256,2048]{0,1:T(8,128)(2,1)S(1)} %copy.127) | copy-start | bytes 3145732
  764.1 90.8 %copy-start.55 = (f32[256]{0:T(256)}, f32[256]{0:T(256)S(1)}, u32[]{:S(2)}) copy-start(f32[256]{0:T(256)S(1)} %broadcast_multiply_fusion.2) | copy-start | bytes 3076
  764.9 16.1 collective-permute-start
  780.9 25.0 %collective-permute-start.1 = (bf16[256,2048]{0,1:T(8,128)(2,1)S(1)}, bf16[256,2048]{0,1:T(8,128)(2,1)S(1)}, u32[]{:S(2)}, u32[]{:S(2)}) collective-permute-start(bf16[256,2048]{0,1:T(8,128)(2,1)S(1)} %collective-permute-done), channel_id=1, source_target_pairs={{0,1},{1,2},{2,3},{3,4},{4,5},{5,6},{6,7},{7,0},{8,9},{9,10},{10,1... | collective-permute-start | bytes 3145736 | tf_op jit(solution)/shard_map/ppermute | solution.py:21
  780.9 25.0 %collective-permute-start.4 = (bf16[256,2048]{0,1:T(8,128)(2,1)S(1)}, bf16[256,2048]{0,1:T(8,128)(2,1)S(1)}, u32[]{:S(2)}, u32[]{:S(2)}) collective-permute-start(bf16[256,2048]{0,1:T(8,128)(2,1)S(1)} %fusion.99), channel_id=1, source_target_pairs={{0,7},{1,0},{2,1},{3,2},{4,3},{5,4},{6,5},{7,6},{8,15},{9,8},{10,9... | collective-permute-start | bytes 3145736 | tf_op jit(solution)/shard_map/ppermute | solution.py:24
  805.9 23.8 %collective-permute-start.2 = (bf16[256,2048]{0,1:T(8,128)(2,1)S(1)}, bf16[256,2048]{0,1:T(8,128)(2,1)}, u32[]{:S(2)}, u32[]{:S(2)}) collective-permute-start(bf16[256,2048]{0,1:T(8,128)(2,1)S(1)} %collective-permute-done.1), channel_id=1, source_target_pairs={{0,1},{1,2},{2,3},{3,4},{4,5},{5,6},{6,7},{7,0},{8,9},{9,10},{10,1... | collective-permute-start | bytes 3145736 | tf_op jit(solution)/shard_map/ppermute | solution.py:21
  806.9 22.9 %collective-permute-start.5 = (bf16[256,2048]{0,1:T(8,128)(2,1)S(1)}, bf16[256,2048]{0,1:T(8,128)(2,1)}, u32[]{:S(2)}, u32[]{:S(2)}) collective-permute-start(bf16[256,2048]{0,1:T(8,128)(2,1)S(1)} %collective-permute-done.4), channel_id=1, source_target_pairs={{0,7},{1,0},{2,1},{3,2},{4,3},{5,4},{6,5},{7,6},{8,15},{9,8},{10,9... | collective-permute-start | bytes 3145736 | tf_op jit(solution)/shard_map/ppermute | solution.py:24
  829.7 23.9 %collective-permute-start.3 = (bf16[256,2048]{0,1:T(8,128)(2,1)}, bf16[256,2048]{0,1:T(8,128)(2,1)}, u32[]{:S(2)}, u32[]{:S(2)}) collective-permute-start(bf16[256,2048]{0,1:T(8,128)(2,1)} %collective-permute-done.2), channel_id=1, source_target_pairs={{0,1},{1,2},{2,3},{3,4},{4,5},{5,6},{6,7},{7,0},{8,9},{9,10},{10,1... | collective-permute-start | bytes 3145736 | tf_op jit(solution)/shard_map/ppermute | solution.py:21
  829.7 26.6 %copy-start.24 = (bf16[256,2048]{0,1:T(8,128)(2,1)S(1)}, bf16[256,2048]{0,1:T(8,128)(2,1)}, u32[]{:S(2)}) copy-start(bf16[256,2048]{0,1:T(8,128)(2,1)} %copy-done.23) | copy-start | bytes 3145732
  829.7 26.9 %copy-start.16 = (bf16[256,2048]{0,1:T(8,128)(2,1)S(1)}, bf16[256,2048]{0,1:T(8,128)(2,1)}, u32[]{:S(2)}) copy-start(bf16[256,2048]{0,1:T(8,128)(2,1)} %copy-done.15) | copy-start | bytes 3145732
  829.8 28.5 %collective-permute-start.6 = (bf16[256,2048]{0,1:T(8,128)(2,1)}, bf16[256,2048]{0,1:T(8,128)(2,1)S(1)}, u32[]{:S(2)}, u32[]{:S(2)}) collective-permute-start(bf16[256,2048]{0,1:T(8,128)(2,1)} %collective-permute-done.5), channel_id=1, source_target_pairs={{0,7},{1,0},{2,1},{3,2},{4,3},{5,4},{6,5},{7,6},{8,15},{9,8},{10,9... | collective-permute-start | bytes 3145736 | tf_op jit(solution)/shard_map/ppermute | solution.py:24
  1021.6 187.2 %copy-start.59 = (f32[64]{0:T(128)S(1)}, f32[64]{0:T(128)}, u32[]{:S(2)}) copy-start(f32[64]{0:T(128)} %copy-done.58) | copy-start | bytes 772
  1021.6 187.5 %copy-start.10 = (bf16[256,2048]{0,1:T(8,128)(2,1)S(1)}, bf16[256,2048]{0,1:T(8,128)(2,1)}, u32[]{:S(2)}) copy-start(bf16[256,2048]{0,1:T(8,128)(2,1)} %fusion.57) | copy-start | bytes 3145732
  1021.6 261.5 %reduce-scatter.19.cloned.1.call-start = ((), (), s32[]{:S(2)}) async-start(), calls=%async_computation.24 | async-start | bytes 1310720 | tf_op jit(solution)/shard_map/reduce_scatter | solution.py:293
  1210.6 72.5 %reduce-scatter.21.cloned.1.call-start = ((), (), s32[]{:S(2)}) async-start(), calls=%async_computation.25 | async-start | bytes 1310720 | tf_op jit(solution)/shard_map/reduce_scatter | solution.py:294
  1212.1 226.3 %reduce-scatter.11.cloned.1.call-start = ((), (), s32[]{:S(2)}) async-start(), calls=%async_computation.19 | async-start | bytes 18874368 | tf_op jit(solution)/shard_map/reduce_scatter | solution.py:228
  1224.9 281.4 %reduce-scatter.29.cloned.1.call-start = ((), (), s32[]{:S(2)}) async-start(), calls=%async_computation.29 | async-start | bytes 7208960 | tf_op jit(solution)/shard_map/reduce_scatter | solution.py:299
  1236.0 339.3 %reduce-scatter.25.cloned.1.call-start = ((), (), s32[]{:S(2)}) async-start(), calls=%async_computation.27 | async-start | bytes 7208960 | tf_op jit(solution)/shard_map/reduce_scatter | solution.py:297
  1247.3 397.2 %reduce-scatter.27.cloned.1.call-start = ((), (), s32[]{:S(2)}) async-start(), calls=%async_computation.28 | async-start | bytes 7208960 | tf_op jit(solution)/shard_map/reduce_scatter | solution.py:298
  1258.5 424.6 %reduce-scatter.17.cloned.1.call-start = ((), (), s32[]{:S(2)}) async-start(), calls=%async_computation.23 | async-start | bytes 2621440 | tf_op jit(solution)/shard_map/reduce_scatter | solution.py:292
  1266.0 455.9 %reduce-scatter.23.cloned.1.call-start = ((), (), s32[]{:S(2)}) async-start(), calls=%async_computation.26 | async-start | bytes 2621440 | tf_op jit(solution)/shard_map/reduce_scatter | solution.py:295
  1275.6 505.1 %all-reduce.7.cloned.1.call-start = ((), (), s32[]{:S(2)}) async-start(), calls=%async_computation.30 | async-start | bytes 1048576 | tf_op jit(solution)/shard_map/psum | solution.py:301
  1279.8 158.6 %copy-start.1 = (f32[256,2048]{0,1:T(8,128)S(1)}, f32[256,2048]{0,1:T(8,128)}, u32[]{:S(2)}) copy-start(f32[256,2048]{0,1:T(8,128)} %copy-done) | copy-start | bytes 6291460
  1279.8 158.6 %copy-start.40 = (f32[4,1,512]{2,1,0:T(1,128)S(1)}, f32[4,1,512]{2,1,0:T(1,128)}, u32[]{:S(2)}) copy-start(f32[4,1,512]{2,1,0:T(1,128)} %copy-done.39) | copy-start | bytes 24580
  1279.8 158.6 %copy-start.52 = (f32[256]{0:T(256)S(1)}, f32[256]{0:T(256)}, u32[]{:S(2)}) copy-start(f32[256]{0:T(256)} %copy-done.51) | copy-start | bytes 3076
  1279.8 158.6 %copy-start.56 = (f32[256]{0:T(256)S(1)}, f32[256]{0:T(256)}, u32[]{:S(2)}) copy-start(f32[256]{0:T(256)} %copy-done.55) | copy-start | bytes 3076
  (53 other events, 497.6 us)
Sparse Core Ops, SparseCore 0:
  10.4 29.0 all-gather.15
  41.7 82.4 all-gather.11
  126.6 24.6 all-gather.13
  152.8 82.0 all-gather.17
  236.5 40.0 all-gather.21
  304.9 80.4 all-gather.19
  387.8 39.7 all-gather.23
  429.4 41.5 all-gather.25
  472.6 82.0 all-gather.27
  594.4 166.6 reduce-scatter.12
  1021.7 186.0 reduce-scatter.14
  1210.7 26.4 reduce-scatter.18
  1240.0 27.8 reduce-scatter.20
  1270.2 168.1 reduce-scatter.10
  1441.8 64.4 reduce-scatter.28
  1509.7 65.6 reduce-scatter.24
  1578.8 65.6 reduce-scatter.26
  1647.9 35.1 reduce-scatter.16
  1686.7 35.1 reduce-scatter.22
  1724.1 56.6 all-reduce.6
